TPU v7x, 32 devices: a whole 2x2x4 slice. The times are simulated.
32 devices in a mesh: group: 2 (over y), win: 16 (over z, x, core).
Axes of the slice: x: 2, y: 2, z: 4, core: 2. Of those that a mesh axis runs over, the one named last changes fastest.
Arguments:
- img_qkv: bfloat16 [64, 256, 4608], P(('group', 'win')), parts along dimension 0, may hold values from -100 to 100
- txt_kv: bfloat16 [64, 128, 3072], P(('group', 'win')), parts along dimension 0, may hold values from -6 to 6
- hidden: bfloat16 [64, 256, 3072], P(('group', 'win')), parts along dimension 0, may hold values from -6 to 6
- w_proj: bfloat16 [1536, 3072], P('win'), may hold values from -0.15625 to 0.15625
- w_out: bfloat16 [3072, 64], replicated, may hold values from -0.109375 to 0.109375
- modulation: float32 [6, 3072], P('group'), parts along dimension 0, may hold values from -3 to 3
- anchors: int32 [64, 2], P(('group', 'win')), parts along dimension 0, may hold values from 0 to 255, as said below
- blend_weight: int32 [64, 32, 32], P(('group', 'win')), parts along dimension 0, may hold values from 0 to 8
Outputs:
- velocity: float32 [16, 512, 64], P(None, ('group', 'win')), parts along dimension 1
There are 2 independent parts, one for each index of `group`. A program takes and returns all parts, laid end to end along the dimension named above; an argument that names none is the same for every part. Nothing has to cross between parts.
Inputs may be any that keep to these rules, and one draw needn't show every extreme that they name: `anchors`: window w's anchor row lies in [16 * (w // 2), 16 * (w // 2) + 16); its columns wrap around the panorama; the 2 windows w with the same w // 2 have anchor columns (s + 32 * (w % 2)) mod 64 for one s of that band, so that they cover all 64 columns.
All inputs are finite; a program needn't handle non-finite values.
Results may differ from a plain program's by a relative error of at most 0.0029.
Values may be sent and summed in bfloat16 or wider, within the bound.
A program may use at most 128 MiB of HBM per device.

v0:
```python
import math

import jax
import jax.numpy as jnp
from jax import lax
from jax.sharding import PartitionSpec as P

HD = 128
C = 16
HEADS = 12
PATCH = 2
WIN = 32
LW = 64
BAND = 16
GRID = 16


def shifted(block, axis, distance):
    devices = range(lax.axis_size(axis))
    route = [(i - distance, i) for i in devices if i - distance in devices]
    return lax.ppermute(block, axis, route)


def place_window(canvas, totals, contrib, weights, row_at, col_at):
    zero_index = jnp.zeros((), jnp.int32)
    region = lax.dynamic_slice(canvas, (zero_index, row_at, col_at), (C, WIN, WIN))
    canvas = lax.dynamic_update_slice(canvas, region + contrib, (zero_index, row_at, col_at))
    weight_region = lax.dynamic_slice(totals, (row_at, col_at), (WIN, WIN))
    totals = lax.dynamic_update_slice(totals, weight_region + weights, (row_at, col_at))
    return (canvas, totals)


def fold_columns(field):
    span_cols = field.shape[-1] - WIN
    leading = field[..., :span_cols]
    wrapped = field[..., span_cols:]
    padding = [(0, 0)] * (field.ndim - 1) + [(0, span_cols - WIN)]
    return leading + jnp.pad(wrapped, padding)


def shards(img_qkv, txt_kv, hidden, w_proj, w_out, modulation, anchors, blend_weight):
    window_count, tokens, _ = img_qkv.shape
    features = HEADS * HD
    queries = img_qkv[:, :, :features].reshape(window_count, tokens, HEADS, HD)
    all_keys = jnp.concatenate(
        [txt_kv[:, :, :features], img_qkv[:, :, features : 2 * features]], axis=1
    )
    all_keys = all_keys.reshape(window_count, -1, HEADS, HD)
    all_values = jnp.concatenate([txt_kv[:, :, features:], img_qkv[:, :, 2 * features :]], axis=1)
    all_values = all_values.reshape(window_count, -1, HEADS, HD)
    scores = jnp.einsum(
        "wqhd,wkhd->whqk", queries, all_keys, preferred_element_type=jnp.float32
    ) / math.sqrt(HD)
    scores = scores - jnp.max(scores, axis=-1, keepdims=True)
    exp_scores = jnp.exp(scores)
    soft_weights = (exp_scores / jnp.sum(exp_scores, axis=-1, keepdims=True)).astype(jnp.bfloat16)
    attended = jnp.einsum(
        "whqk,wkhd->wqhd", soft_weights, all_values, preferred_element_type=jnp.float32
    )
    attended = attended.reshape(window_count * tokens, features).astype(jnp.bfloat16)
    whole_proj = lax.all_gather(w_proj, "win", axis=0, tiled=True)
    projected = jnp.dot(attended, whole_proj, preferred_element_type=jnp.float32)
    residual = (
        hidden.reshape(window_count * tokens, -1).astype(jnp.float32) + modulation[0] * projected
    )
    row_mean = jnp.mean(residual, axis=-1, keepdims=True)
    centred = residual - row_mean
    row_var = jnp.mean(centred * centred, axis=-1, keepdims=True)
    normed = centred * lax.rsqrt(row_var + 1e-06)
    modulated = (normed * (1.0 + modulation[1]) + modulation[2]).astype(jnp.bfloat16)
    patch_vel = jnp.dot(modulated, w_out, preferred_element_type=jnp.float32)
    patch_grid = patch_vel.reshape(window_count, GRID, GRID, C, PATCH, PATCH)
    window_vel = patch_grid.transpose(0, 3, 1, 4, 2, 5).reshape(window_count, C, WIN, WIN)
    weights = blend_weight.astype(jnp.float32)
    contrib = window_vel * weights[:, None]
    band_start = lax.axis_index("win") * BAND
    canvas = jnp.zeros((C, BAND + WIN, LW + WIN), jnp.float32)
    totals = jnp.zeros((BAND + WIN, LW + WIN), jnp.float32)

    def add_one(window, running):
        row_at = anchors[window, 0] - band_start
        col_at = anchors[window, 1]
        return place_window(
            running[0], running[1], contrib[window], weights[window], row_at, col_at
        )

    canvas, totals = lax.fori_loop(0, window_count, add_one, (canvas, totals))
    canvas = fold_columns(canvas)
    totals = fold_columns(totals)
    own_canvas = canvas[:, :BAND]
    own_totals = totals[:BAND]
    near_canvas = canvas[:, BAND : 2 * BAND]
    near_totals = totals[BAND : 2 * BAND]
    far_canvas = canvas[:, 2 * BAND :]
    far_totals = totals[2 * BAND :]
    prev_canvas, prev_totals = shifted((near_canvas, near_totals), "win", 1)
    second_canvas, second_totals = shifted((far_canvas, far_totals), "win", 2)
    sum_canvas = own_canvas + prev_canvas + second_canvas
    sum_totals = own_totals + prev_totals + second_totals
    return sum_canvas / jnp.maximum(sum_totals, 1.0)[None]


def solution(mesh):
    in_specs = (
        P(("group", "win"), None, None),
        P(("group", "win"), None, None),
        P(("group", "win"), None, None),
        P("win", None),
        P(),
        P("group", None),
        P(("group", "win"), None),
        P(("group", "win"), None, None),
    )
    out_specs = P(None, ("group", "win"), None)
    return jax.shard_map(shards, mesh=mesh, in_specs=in_specs, out_specs=out_specs, check_vma=False)
```

profile of v0, /device:TPU:8, one launch (start us, length us, event | category | flops | bytes accessed | tf_op | source)
XLA Modules:
  0.0 151.4 jit_solution(16014188008691737487)
XLA Ops:
  6.5 0.7 all-gather.2.cloned.1.call-update
  7.3 3.9 %fusion.18 = (bf16[2,256,1536]{2,1,0:T(8,128)(2,1)S(1)}, bf16[2,256,1536]{2,1,0:T(8,128)(2,1)S(1)}, bf16[2,256,1536]{2,1,0:T(8,128)(2,1)}) fusion(bf16[2,256,4608]{2,1,0:T(8,128)(2,1)} %param.10), kind=kLoop, calls=%fused_computation.35 | loop fusion | bytes 9437184 | tf_op jit(solution)/shard_map/slice | solution.py:44
  11.2 1.6 %copy.26 = bf16[2,256,1536]{1,2,0:T(8,128)(2,1)} copy(bf16[2,256,1536]{2,1,0:T(8,128)(2,1)S(1)} %get-tuple-element.156) | data formatting | bytes 3145728
  12.8 2.4 %fusion.19 = (bf16[2,128,1536]{2,1,0:T(8,128)(2,1)S(1)}, bf16[2,128,1536]{2,1,0:T(8,128)(2,1)}) fusion(bf16[2,128,3072]{2,1,0:T(8,128)(2,1)} %param.11), kind=kLoop, calls=%fused_computation.36 | loop fusion | bytes 3145728 | tf_op jit(solution)/shard_map/slice | solution.py:46
  15.2 0.4 copy.25
  15.6 1.6 %copy.27 = bf16[2,256,1536]{1,2,0:T(8,128)(2,1)} copy(bf16[2,256,1536]{2,1,0:T(8,128)(2,1)S(1)} %get-tuple-element.155) | data formatting | bytes 3145728
  17.2 1.9 %pad_maximum_fusion = bf16[2,384,1536]{2,1,0:T(8,128)(2,1)S(1)} fusion(bf16[2,256,1536]{2,1,0:T(8,128)(2,1)} %get-tuple-element.157, bf16[2,128,1536]{2,1,0:T(8,128)(2,1)} %get-tuple-element.159), kind=kLoop, calls=%fused_computation.17 | loop fusion | flops 4718592 | bytes 4718592 | tf_op jit(solution)/shard_map/concatenate | solution.py:49
  19.1 2.5 %copy.12 = bf16[2,384,1536]{1,2,0:T(8,128)(2,1)} copy(bf16[2,384,1536]{2,1,0:T(8,128)(2,1)S(1)} %pad_maximum_fusion) | data formatting | bytes 4718592 | tf_op jit(solution)/shard_map/concatenate | solution.py:49
  21.6 3.2 %pad_maximum_fusion.1 = bf16[2,384,1536]{1,2,0:T(8,128)(2,1)} fusion(bf16[2,256,1536]{1,2,0:T(8,128)(2,1)} %copy.26, bf16[2,128,1536]{1,2,0:T(8,128)(2,1)S(1)} %copy.25), kind=kLoop, calls=%fused_computation.18 | loop fusion | flops 4718592 | bytes 4718592 | tf_op jit(solution)/shard_map/concatenate | solution.py:45
  24.8 9.2 %fusion.22 = (f32[2,12,256]{2,1,0:T(8,128)S(1)}, f32[2,12,256,384]{2,3,1,0:T(8,128)}) fusion(bf16[2,384,12,128]{1,3,2,0:T(8,128)(2,1)} %bitcast.56, bf16[2,256,12,128]{1,3,2,0:T(8,128)(2,1)} %bitcast.58), kind=kOutput, calls=%fused_computation.39 | convolution fusion | flops 611058048 | bytes 13393920 | tf_op jit(solution)/shard_map/sub | solution.py:54
  34.0 4.7 %fusion.10 = bf16[2,256,12,128]{1,3,2,0:T(8,128)(2,1)S(1)} fusion(bf16[2,384,12,128]{1,3,2,0:T(8,128)(2,1)S(1)} %bitcast.55, f32[2,12,256,384]{2,3,1,0:T(8,128)} %get-tuple-element.168, f32[2,12,256]{2,1,0:T(8,128)S(1)} %get-tuple-element.167), kind=kOutput, calls=%fused_computation.20 | convolution fusion | flops 609484800 | bytes 13393920 | tf_op jit(solution)/shard_map/whqk,wkhd->wqhd/dot_general | solution.py:57
  38.7 0.0 copy-start.2
  38.8 0.0 copy-start.3
  38.8 1.6 %copy.19 = bf16[2,256,12,128]{1,0,3,2:T(2,128)(2,1)S(1)} copy(bf16[2,256,12,128]{1,3,2,0:T(8,128)(2,1)S(1)} %fusion.10) | data formatting | bytes 3145728 | tf_op jit(solution)/shard_map/convert_element_type | solution.py:60
  40.4 0.3 copy.28
  40.7 0.6 convert_element_type.35
  41.4 49.8 %all-gather.2.cloned.1.call-done = bf16[1536,3072]{1,0:T(8,128)(2,1)} async-done(((bf16[96,3072]{1,0:T(8,128)(2,1)}), bf16[1536,3072]{1,0:T(8,128)(2,1)}) %all-gather.2.cloned.1.call-update) | async-done | bytes 9437200 | tf_op jit(solution)/shard_map/all_gather | solution.py:61
  91.2 8.9 %fusion.23 = (f32[512]{0:T(512)S(1)}, f32[512,3072]{1,0:T(8,128)S(1)}) fusion(bf16[512,1536]{0,1:T(8,128)(2,1)S(1)} %bitcast.57, bf16[1536,3072]{1,0:T(8,128)(2,1)} %all-gather.2.cloned.1.call-done, f32[3072]{0:T(1024)S(1)} %bitcast.61, bf16[512,3072]{1,0:T(8,128)(2,1)} %bitcast.62), kind=kOutput, calls=%fused_computation.40 | convolution fusion | flops 4838129152 | bytes 20461568 | tf_op jit(solution)/shard_map/dot_general | solution.py:62
  100.2 0.8 multiply_reduce_fusion
  100.9 1.4 fusion.8
  102.4 0.0 copy-start.4
  102.4 0.4 reshape.39
  102.8 0.8 copy.20
  103.6 1.1 broadcast_multiply_fusion
  104.7 0.5 copy.21
  105.2 21.3 %while.15 = (s32[]{:T(128)}, f32[16,48,96]{2,1,0:T(8,128)S(1)}, f32[48,96]{1,0:T(8,128)S(1)}, s32[2,2]{1,0:T(2,128)S(1)}, s32[]{:T(128)}, /*index=5*/f32[2,16,32...) while((s32[]{:T(128)}, f32[16,48,96]{2,1,0:T(8,128)S(1)}, ...), condition=%wide.region_5.0_spmd, body=%wide.region_4.0_spmd.sunk | while | flops 17417 | bytes 348401 | solution.py:87
  105.2 0.6 constant_dynamic-slice_fusion.3
  108.4 0.1 bitcast_add_fusion.4
  108.5 5.7 %dynamic_update_slice.16 = f32[16,48,96]{2,1,0:T(8,128)S(1)} dynamic-update-slice(f32[16,48,96]{2,1,0:T(8,128)S(1)} %get-tuple-element.230, f32[16,32,32]{2,1,0:T(8,128)S(1)} %bitcast_add_fusion.4, s32[]{:T(128)} %constant.52.clone.1..sunk, s32[]{:T(128)S(6)} %select_n.30, s32[]{:T(128)S(6)} %select_n.31) | dynamic-update-slice | bytes 131076 | tf_op jit(solution)/shard_map/while/body/eval_jaxpr/dynamic_update_slice | solution.py:27
  114.2 0.8 bitcast_add_fusion.5
  115.0 0.8 dynamic_update_slice.17
  115.9 0.6 constant_dynamic-slice_fusion.3
  119.0 0.1 bitcast_add_fusion.4
  119.2 5.7 %dynamic_update_slice.16 = f32[16,48,96]{2,1,0:T(8,128)S(1)} dynamic-update-slice(f32[16,48,96]{2,1,0:T(8,128)S(1)} %get-tuple-element.230, f32[16,32,32]{2,1,0:T(8,128)S(1)} %bitcast_add_fusion.4, s32[]{:T(128)} %constant.52.clone.1..sunk, s32[]{:T(128)S(6)} %select_n.30, s32[]{:T(128)S(6)} %select_n.31) | dynamic-update-slice | bytes 131076 | tf_op jit(solution)/shard_map/while/body/eval_jaxpr/dynamic_update_slice | solution.py:27
  124.9 0.8 bitcast_add_fusion.5
  125.7 0.8 dynamic_update_slice.17
  126.5 0.1 slice.68
  126.6 2.1 %collective-permute-start.2 = (f32[16,64]{1,0:T(8,128)S(1)}, f32[16,64]{1,0:T(8,128)S(1)}, u32[]{:S(2)}, u32[]{:S(2)}) collective-permute-start(f32[16,64]{1,0:T(8,128)S(1)} %get-tuple-element.165), channel_id=1, source_target_pairs={{0,1},{1,2},{2,3},{3,4},{4,5},{5,6},{6,7},{7,8},{8,9},{9,10},{10,1... | collective-permute-start | bytes 12296 | tf_op jit(solution)/shard_map/ppermute | solution.py:21
  128.7 2.2 %collective-permute-start.3 = (f32[16,64]{1,0:T(8,128)S(1)}, f32[16,64]{1,0:T(8,128)S(1)}, u32[]{:S(2)}, u32[]{:S(2)}) collective-permute-start(f32[16,64]{1,0:T(8,128)S(1)} %get-tuple-element.166), channel_id=1, source_target_pairs={{0,2},{1,3},{2,4},{3,5},{4,6},{5,7},{6,8},{7,9},{8,10},{9,11},{10,... | collective-permute-start | bytes 12296 | tf_op jit(solution)/shard_map/ppermute | solution.py:21
  131.0 0.2 slice.63
  131.2 0.1 pad_add_fusion
  131.2 3.9 %collective-permute-start = (f32[16,16,64]{2,1,0:T(8,128)S(1)}, f32[16,16,64]{2,1,0:T(8,128)S(1)}, u32[]{:S(2)}, u32[]{:S(2)}) collective-permute-start(f32[16,16,64]{2,1,0:T(8,128)S(1)} %get-tuple-element.160), channel_id=1, source_target_pairs={{0,1},{1,2},{2,3},{3,4},{4,5},{5,6},{6,7},{7,8},{8,9},{9,10},{10,1... | collective-permute-start | bytes 196616 | tf_op jit(solution)/shard_map/ppermute | solution.py:21
  135.2 2.4 %collective-permute-start.1 = (f32[16,16,64]{2,1,0:T(8,128)S(1)}, f32[16,16,64]{2,1,0:T(8,128)S(1)}, u32[]{:S(2)}, u32[]{:S(2)}) collective-permute-start(f32[16,16,64]{2,1,0:T(8,128)S(1)} %get-tuple-element.161), channel_id=1, source_target_pairs={{0,2},{1,3},{2,4},{3,5},{4,6},{5,7},{6,8},{7,9},{8,10},{9,11},{10,... | collective-permute-start | bytes 196616 | tf_op jit(solution)/shard_map/ppermute | solution.py:21
  137.6 0.0 collective-permute-done.2
  137.6 0.0 collective-permute-done.3
  137.6 0.8 collective-permute-done
  138.4 5.4 %collective-permute-done.1 = f32[16,16,64]{2,1,0:T(8,128)S(1)} collective-permute-done((f32[16,16,64]{2,1,0:T(8,128)S(1)}, f32[16,16,64]{2,1,0:T(8,128)S(1)}, u32[]{:S(2)}, u32[]{:S(2)}) %collective-permute-start.1) | collective-permute-done | bytes 65568 | tf_op jit(solution)/shard_map/ppermute | solution.py:21
  143.9 0.7 fusion.14
  (17 shorter events, 0.1 us)
Async XLA Ops:
  6.5 94.4 %copy-start = (bf16[3072,64]{0,1:T(8,128)(2,1)S(1)}, bf16[3072,64]{0,1:T(8,128)(2,1)}, u32[]{:S(2)}) copy-start(bf16[3072,64]{0,1:T(8,128)(2,1)} %param.14) | copy-start | bytes 1179652
  6.5 84.7 %all-gather.2.cloned.1.call-start = ((), (), s32[]{:S(2)}) async-start(), calls=%async_computation | async-start | bytes 10027008 | tf_op jit(solution)/shard_map/all_gather | solution.py:61
  24.8 9.2 %copy-start.1 = (bf16[2,384,1536]{1,2,0:T(8,128)(2,1)S(1)}, bf16[2,384,1536]{1,2,0:T(8,128)(2,1)}, u32[]{:S(2)}) copy-start(bf16[2,384,1536]{1,2,0:T(8,128)(2,1)} %copy.12) | copy-start | bytes 7077892
  38.7 2.0 %copy-start.2 = (s32[2,32,32]{2,1,0:T(8,128)S(1)}, s32[2,32,32]{2,1,0:T(8,128)}, u32[]{:S(2)}) copy-start(s32[2,32,32]{2,1,0:T(8,128)} %param.17) | copy-start | bytes 24580
  38.8 2.6 %copy-start.3 = (f32[3,3072]{1,0:T(4,128)S(1)}, f32[3,3072]{1,0:T(4,128)}, u32[]{:S(2)}) copy-start(f32[3,3072]{1,0:T(4,128)} %param.15) | copy-start | bytes 110596
  102.4 2.8 %copy-start.4 = (s32[2,2]{1,0:T(2,128)S(1)}, s32[2,2]{1,0:T(2,128)}, u32[]{:S(2)}) copy-start(s32[2,2]{1,0:T(2,128)} %param.16) | copy-start | bytes 52
  126.6 11.0 %collective-permute-start.2 = (f32[16,64]{1,0:T(8,128)S(1)}, f32[16,64]{1,0:T(8,128)S(1)}, u32[]{:S(2)}, u32[]{:S(2)}) collective-permute-start(f32[16,64]{1,0:T(8,128)S(1)} %get-tuple-element.165), channel_id=1, source_target_pairs={{0,1},{1,2},{2,3},{3,4},{4,5},{5,6},{6,7},{7,8},{8,9},{9,10},{10,1... | collective-permute-start | bytes 12296 | tf_op jit(solution)/shard_map/ppermute | solution.py:21
  128.7 8.9 %collective-permute-start.3 = (f32[16,64]{1,0:T(8,128)S(1)}, f32[16,64]{1,0:T(8,128)S(1)}, u32[]{:S(2)}, u32[]{:S(2)}) collective-permute-start(f32[16,64]{1,0:T(8,128)S(1)} %get-tuple-element.166), channel_id=1, source_target_pairs={{0,2},{1,3},{2,4},{3,5},{4,6},{5,7},{6,8},{7,9},{8,10},{9,11},{10,... | collective-permute-start | bytes 12296 | tf_op jit(solution)/shard_map/ppermute | solution.py:21
  131.2 7.2 %collective-permute-start = (f32[16,16,64]{2,1,0:T(8,128)S(1)}, f32[16,16,64]{2,1,0:T(8,128)S(1)}, u32[]{:S(2)}, u32[]{:S(2)}) collective-permute-start(f32[16,16,64]{2,1,0:T(8,128)S(1)} %get-tuple-element.160), channel_id=1, source_target_pairs={{0,1},{1,2},{2,3},{3,4},{4,5},{5,6},{6,7},{7,8},{8,9},{9,10},{10,1... | collective-permute-start | bytes 196616 | tf_op jit(solution)/shard_map/ppermute | solution.py:21
  135.2 8.7 %collective-permute-start.1 = (f32[16,16,64]{2,1,0:T(8,128)S(1)}, f32[16,16,64]{2,1,0:T(8,128)S(1)}, u32[]{:S(2)}, u32[]{:S(2)}) collective-permute-start(f32[16,16,64]{2,1,0:T(8,128)S(1)} %get-tuple-element.161), channel_id=1, source_target_pairs={{0,2},{1,3},{2,4},{3,5},{4,6},{5,7},{6,8},{7,9},{8,10},{9,11},{10,... | collective-permute-start | bytes 196616 | tf_op jit(solution)/shard_map/ppermute | solution.py:21
Sparse Core Ops, SparseCore 0:
  9.6 81.5 all-gather.1
where the time goes:
time: 152 us; the launch traced here: 151 us
  waiting for transfers between devices  56.8 us (37%)
  local copies, waits for them, and re-layouts  30.6 us (20%)
  matrix products  24.3 us (16%)
  between operations  13.6 us (9%)
  starting transfers between devices  10.7 us (7%)
  other arithmetic  10.3 us (7%)
  loops' own time  5.12 us (3%)
    all_gather x1, waiting for transfers between devices, shards(): whole_proj = lax.all_gather(w_proj, 'win', axis=0, tiled=True)  49.8 us
    dynamic_update_slice x2, local copies, waits for them, and re-layouts, place_window(): lax.dynamic_update_slice(canvas, region + contrib, (zero_index, row_at, c...  11.4 us
    ppermute x4, starting transfers between devices, shifted(): return lax.ppermute(block, axis, route)  10.7 us
    sub x1, matrix products, shards(): scores = scores - jnp.max(scores, axis=-1, keepdims=True)  9.21 us
    dot_general x1, matrix products, shards(): jnp.dot(attended, whole_proj, preferred_element_type=jnp.float32)  8.95 us
    ppermute x4, waiting for transfers between devices, shifted(): return lax.ppermute(block, axis, route)  6.25 us
    another operation x1, loops' own time, shards(): canvas, totals = lax.fori_loop(0, window_count, add_one, (canvas, totals))  5.12 us
    dot_general x1, matrix products, shards(): jnp.einsum('whqk,wkhd->wqhd', soft_weights, all_values, preferred_element...  4.71 us
  transfers between devices with their start and end apart: 5, of which 3 were waited for; matrix products, arithmetic and copies ran while one was open for 23% of the time, Pallas kernels for 0%

commit v1 on v0

--- a/solution.py
+++ b/solution.py
@@ -1,8 +1,11 @@
+import functools
 import math
 
 import jax
 import jax.numpy as jnp
 from jax import lax
+from jax.experimental import pallas as pl
+from jax.experimental.pallas import tpu as pltpu
 from jax.sharding import PartitionSpec as P
 
 HD = 128
@@ -38,7 +41,7 @@
     return leading + jnp.pad(wrapped, padding)
 
 
-def shards(img_qkv, txt_kv, hidden, w_proj, w_out, modulation, anchors, blend_weight):
+def plain_shards(img_qkv, txt_kv, hidden, w_proj, w_out, modulation, anchors, blend_weight):
     window_count, tokens, _ = img_qkv.shape
     features = HEADS * HD
     queries = img_qkv[:, :, :features].reshape(window_count, tokens, HEADS, HD)
@@ -100,6 +103,316 @@
     return sum_canvas / jnp.maximum(sum_totals, 1.0)[None]
 
 
+LOG2E = 1.4426950408889634
+MESH_ID = pl.DeviceIdType.MESH
+
+
+def block_kernel(
+    n,
+    qkv_hbm,
+    txt_hbm,
+    hid_hbm,
+    wp_hbm,
+    wout_ref,
+    mod_ref,
+    out_ref,
+    qkv,
+    txt,
+    hid,
+    weights,
+    att,
+    lhs,
+    acc,
+    load_sems,
+    cw_send,
+    cw_recv,
+    ccw_send,
+    ccw_recv,
+    y_send,
+    y_recv,
+    own_sems,
+    part_send,
+    part_recv,
+):
+    windows, tokens, _ = qkv.shape
+    text = txt.shape[1]
+    rows = wp_hbm.shape[0]
+    width = weights.shape[1]
+    features = HEADS * HD
+    third = width // 3
+    half = third // 2
+    chips = n // 2
+    length = chips // 2
+    group = lax.axis_index("group")
+    me = lax.axis_index("win")
+    core = me % 2
+    chip = me // 2
+    depth, side = chip // 2, chip % 2
+    place = depth + side * (chips - 1 - 2 * depth)
+
+    def chip_at(position):
+        spot = (position + chips) % chips
+        turn = spot // length
+        return 2 * (spot + turn * (chips - 1 - 2 * spot)) + turn
+
+    def ranked(which_chip, which_core):
+        return which_chip * 2 + which_core
+
+    onward = (group, ranked(chip_at(place + 1), core))
+    backward = (group, ranked(chip_at(place - 1), core))
+    across = (1 - group, me)
+    partner = (group, me + 1 - 2 * core)
+    own_third = group * (2 * third)
+    far_third = (1 - group) * (2 * third)
+
+    def region(which_chip, which_core, col, cols):
+        row = pl.multiple_of(ranked(which_chip, which_core) * rows, 16)
+        return weights.at[pl.ds(row, rows), pl.ds(pl.multiple_of(col, 128), cols)]
+
+    def remote(ref, send, recv, device):
+        return pltpu.make_async_remote_copy(
+            src_ref=ref, dst_ref=ref, send_sem=send, recv_sem=recv,
+            device_id=device, device_id_type=MESH_ID,
+        )
+
+    def cw(step, sub, hop):
+        ref = region(chip_at(place - step - hop), core, own_third + sub * half, half)
+        return remote(ref, cw_send.at[step, sub], cw_recv.at[step, sub], onward)
+
+    def ccw(step, sub, hop):
+        ref = region(chip_at(place + step + hop), core, third + sub * half, half)
+        return remote(ref, ccw_send.at[step, sub], ccw_recv.at[step, sub], backward)
+
+    def yy(step, sub, col):
+        ref = region(chip_at(place - step - 1), core, col + sub * half, half)
+        return remote(ref, y_send.at[step, sub], y_recv.at[step, sub], across)
+
+    def part(step, kind, which_core):
+        col = (own_third, third, far_third)[kind]
+        source = chip_at(place + step + 1) if kind == 1 else chip_at(place - step - 1)
+        ref = region(source, which_core, col, third)
+        return remote(ref, part_send.at[step, kind], part_recv.at[step, kind], partner)
+
+    def part_own(which_core):
+        ref = region(chip, which_core, 0, width)
+        return remote(ref, own_sems.at[0], own_sems.at[1], partner)
+
+    own_load = pltpu.make_async_copy(wp_hbm, region(chip, core, 0, width), load_sems.at[0])
+    own_load.start()
+    loads = []
+    for w in range(windows):
+        loads.append(
+            (
+                pltpu.make_async_copy(qkv_hbm.at[w], qkv.at[w], load_sems.at[1 + 2 * w]),
+                pltpu.make_async_copy(txt_hbm.at[w], txt.at[w], load_sems.at[2 + 2 * w]),
+            )
+        )
+    hid_load = pltpu.make_async_copy(hid_hbm, hid, load_sems.at[1 + 2 * windows])
+    for pair in loads:
+        for copy in pair:
+            copy.start()
+    hid_load.start()
+
+    barrier = pltpu.get_barrier_semaphore()
+    for device in (onward, backward, across, partner):
+        pl.semaphore_signal(barrier, inc=1, device_id=device, device_id_type=MESH_ID)
+    pl.semaphore_wait(barrier, 4)
+
+    own_load.wait()
+    for sub in range(2):
+        cw(0, sub, 0).start()
+        ccw(0, sub, 0).start()
+    part_own(core).start()
+
+    scale = LOG2E / math.sqrt(HD)
+
+    def attend(w, h):
+        col = pl.multiple_of(h * HD, HD)
+        cols = pl.ds(col, HD)
+        kcols = pl.ds(pl.multiple_of(col + features, HD), HD)
+        vcols = pl.ds(pl.multiple_of(col + 2 * features, HD), HD)
+        q = qkv[w, :, cols]
+        dims = (((1,), (1,)), ((), ()))
+        st = lax.dot_general(txt[w, :, cols], q, dims, preferred_element_type=jnp.float32)
+        si = lax.dot_general(qkv[w, :, kcols], q, dims, preferred_element_type=jnp.float32)
+        top = jnp.maximum(jnp.max(st, axis=0, keepdims=True), jnp.max(si, axis=0, keepdims=True))
+        pt = jnp.exp2((st - top) * scale)
+        pi = jnp.exp2((si - top) * scale)
+        total = jnp.sum(pt, axis=0, keepdims=True) + jnp.sum(pi, axis=0, keepdims=True)
+        back = (((0,), (0,)), ((), ()))
+        out = lax.dot_general(
+            txt[w, :, kcols], pt.astype(jnp.bfloat16), back, preferred_element_type=jnp.float32
+        ) + lax.dot_general(
+            qkv[w, :, vcols], pi.astype(jnp.bfloat16), back, preferred_element_type=jnp.float32
+        )
+        att[pl.ds(col, HD), pl.ds(pl.multiple_of(w * tokens, 128), tokens)] = (
+            out * (1.0 / total)
+        ).astype(jnp.bfloat16)
+
+    tile = 256 if third % 256 == 0 else third
+
+    def project(left_chip, col, cols, first=False):
+        row = pl.multiple_of(left_chip * (2 * rows), 16)
+        lhs[...] = att[pl.ds(row, 2 * rows), :].T
+
+        def one(t, carry):
+            at = pl.ds(pl.multiple_of(col + t * tile, 128), tile)
+            term = jnp.dot(
+                lhs[...], weights[pl.ds(row, 2 * rows), at], preferred_element_type=jnp.float32
+            )
+            acc[:, at] = term if first else acc[:, at] + term
+            return carry
+
+        lax.fori_loop(0, cols // tile, one, 0)
+
+    def project_step(step):
+        for kind in range(3):
+            part(step, kind, 1 - core).wait_recv()
+        project(chip_at(place - step - 1), own_third, third)
+        project(chip_at(place - step - 1), far_third, third)
+        project(chip_at(place + step + 1), third, third)
+
+    def serve(step, sub, more):
+        cw(step, sub, 1).wait_recv()
+        if more:
+            cw(step + 1, sub, 0).start()
+        yy(step, sub, own_third).start()
+        ccw(step, sub, 1).wait_recv()
+        if more:
+            ccw(step + 1, sub, 0).start()
+
+    def hand_over(step):
+        part(step, 0, core).start()
+        part(step, 1, core).start()
+
+    def hand_across(step):
+        for sub in range(2):
+            yy(step, sub, far_third).wait_recv()
+        part(step, 2, core).start()
+
+    steps = chips - 1
+    early = (steps + 1) // 2
+    slots = 2 * early
+    units = windows * HEADS
+    per = -(-units // slots)
+    done = 0
+    plan = []
+    for slot in range(slots):
+        plan.append(range(done, min(units, done + per)))
+        done = min(units, done + per)
+    ready = set()
+    for step in range(early):
+        for sub in range(2):
+            for unit in plan[2 * step + sub]:
+                w, h = unit // HEADS, unit % HEADS
+                if w not in ready:
+                    for copy in loads[w]:
+                        copy.wait()
+                    ready.add(w)
+                attend(w, h)
+            serve(step, sub, step + 1 < steps)
+        hand_over(step)
+        if step >= 1:
+            hand_across(step - 1)
+    part_own(1 - core).wait_recv()
+    project(chip, 0, width, first=True)
+    due = 0
+    for step in range(early, steps):
+        for sub in range(2):
+            if due <= step - 2:
+                project_step(due)
+                due += 1
+            serve(step, sub, step + 1 < steps)
+        hand_over(step)
+        hand_across(step - 1)
+    hand_across(steps - 1)
+    while due < steps:
+        project_step(due)
+        due += 1
+
+    hid_load.wait()
+    block = 64 if acc.shape[0] % 64 == 0 else acc.shape[0]
+    gate = mod_ref[0:1, :]
+    gain = 1.0 + mod_ref[1:2, :]
+    shift = mod_ref[2:3, :]
+
+    def norm(b, carry):
+        at = pl.ds(pl.multiple_of(b * block, 16), block)
+        residual = hid[at, :].astype(jnp.float32) + gate * acc[at, :]
+        mean = jnp.sum(residual, axis=-1, keepdims=True) * (1.0 / width)
+        centred = residual - mean
+        var = jnp.sum(centred * centred, axis=-1, keepdims=True) * (1.0 / width)
+        modulated = (centred * lax.rsqrt(var + 1e-06) * gain + shift).astype(jnp.bfloat16)
+        out_ref[at, :] = jnp.dot(modulated, wout_ref[...], preferred_element_type=jnp.float32)
+        return carry
+
+    lax.fori_loop(0, acc.shape[0] // block, norm, 0)
+
+    for step in range(steps):
+        for sub in range(2):
+            cw(step, sub, 0).wait_send()
+            ccw(step, sub, 0).wait_send()
+            yy(step, sub, own_third).wait_send()
+        for kind in range(3):
+            part(step, kind, core).wait_send()
+    part_own(core).wait_send()
+
+
+def shards(n, img_qkv, txt_kv, hidden, w_proj, w_out, modulation, anchors, blend_weight):
+    windows, tokens, qkv_width = img_qkv.shape
+    rows, width = w_proj.shape
+    total = windows * tokens
+    steps = n // 2 - 1
+    any_space = pl.BlockSpec(memory_space=pl.ANY)
+    vmem = pl.BlockSpec(memory_space=pltpu.VMEM)
+    dma = pltpu.SemaphoreType.DMA
+    patch_vel = pl.pallas_call(
+        functools.partial(block_kernel, n),
+        out_shape=jax.ShapeDtypeStruct((total, w_out.shape[1]), jnp.float32),
+        in_specs=[any_space] * 4 + [vmem] * 2,
+        out_specs=vmem,
+        scratch_shapes=[
+            pltpu.VMEM(img_qkv.shape, jnp.bfloat16),
+            pltpu.VMEM(txt_kv.shape, jnp.bfloat16),
+            pltpu.VMEM((total, width), jnp.bfloat16),
+            pltpu.VMEM((n * rows, width), jnp.bfloat16),
+            pltpu.VMEM((n * rows, total), jnp.bfloat16),
+            pltpu.VMEM((total, 2 * rows), jnp.bfloat16),
+            pltpu.VMEM((total, width), jnp.float32),
+            dma((2 + 2 * windows,)),
+            dma((steps, 2)),
+            dma((steps, 2)),
+            dma((steps, 2)),
+            dma((steps, 2)),
+            dma((steps, 2)),
+            dma((steps, 2)),
+            dma((2,)),
+            dma((steps, 3)),
+            dma((steps, 3)),
+        ],
+        compiler_params=pltpu.CompilerParams(
+            collective_id=0, has_side_effects=True, vmem_limit_bytes=60 * 1024 * 1024
+        ),
+    )(img_qkv, txt_kv, hidden.reshape(total, width), w_proj, w_out, modulation)
+
+    weights = blend_weight.astype(jnp.float32)
+    grid = patch_vel.reshape(windows, GRID, GRID, C, PATCH, PATCH)
+    window_vel = grid.transpose(0, 3, 1, 4, 2, 5).reshape(windows, C, WIN, WIN)
+    contrib = jnp.concatenate([window_vel * weights[:, None], weights[:, None]], axis=1)
+    band_start = lax.axis_index("win") * BAND
+    cells = jnp.arange(WIN, dtype=jnp.int32)
+    row_of = anchors[:, 0:1] - band_start + cells
+    col_of = (anchors[:, 1:2] + cells) % LW
+    row_hot = (row_of[:, :, None] == jnp.arange(BAND + WIN, dtype=jnp.int32)).astype(jnp.float32)
+    col_hot = (col_of[:, :, None] == jnp.arange(LW, dtype=jnp.int32)).astype(jnp.float32)
+    wide = jnp.einsum("wcab,wbs->wcas", contrib, col_hot, precision=lax.Precision.HIGHEST)
+    canvas = jnp.einsum("wcas,war->crs", wide, row_hot, precision=lax.Precision.HIGHEST)
+    near = shifted(canvas[:, BAND : 2 * BAND], "win", 1)
+    far = shifted(canvas[:, 2 * BAND :], "win", 2)
+    summed = canvas[:, :BAND] + near + far
+    return summed[:C] / jnp.maximum(summed[C], 1.0)[None]
+
+
 def solution(mesh):
     in_specs = (
         P(("group", "win"), None, None),
@@ -112,4 +425,13 @@
         P(("group", "win"), None, None),
     )
     out_specs = P(None, ("group", "win"), None)
-    return jax.shard_map(shards, mesh=mesh, in_specs=in_specs, out_specs=out_specs, check_vma=False)
+    n = mesh.shape["win"]
+
+    def body(*args):
+        rows, width = args[3].shape
+        ringed = mesh.shape["group"] == 2 and n % 4 == 0 and rows % 16 == 0 and width % 768 == 0
+        if ringed:
+            return shards(n, *args)
+        return plain_shards(*args)
+
+    return jax.shard_map(body, mesh=mesh, in_specs=in_specs, out_specs=out_specs, check_vma=False)

time: 152 us -> 80.6 us (0.53)
  Pallas kernels: 0 us -> 62 us
  waiting for transfers between devices: 56.8 us -> 5.5 us
  local copies, waits for them, and re-layouts: 30.6 us -> 4.88 us
  matrix products: 24.3 us -> 0.88 us
  between operations: 13.6 us -> 0.13 us
  other arithmetic: 10.3 us -> 1.76 us
  starting transfers between devices: 10.7 us -> 5.17 us
  loops' own time: 5.12 us -> 0 us
    pallas_call x0 -> x1, Pallas kernels: none -> 62 us  [shards(): pl.pallas_call(functools.partial(block_kernel, n), out_shape=jax.ShapeDty...]
    all_gather x1 -> x0, waiting for transfers between devices: 49.8 us -> none  [shards(): whole_proj = lax.all_gather(w_proj, 'win', axis=0, tiled=True)]
    dot_general x3 -> x2, matrix products: 15.1 us -> 0.88 us  [the longest x1 0.44 us: shards(): jnp.einsum('wcab,wbs->wcas', contrib, col_hot, precision=lax.Precision.HI...]
    dynamic_update_slice x4 -> x0, local copies, waits for them, and re-layouts: 13 us -> none  [the longest x2 11.4 us: place_window(): lax.dynamic_update_slice(canvas, region + contrib, (zero_index, row_at, c...]
    sub x1 -> x0, matrix products: 9.21 us -> none  [shards(): scores = scores - jnp.max(scores, axis=-1, keepdims=True)]
    slice x6 -> x1, local copies, waits for them, and re-layouts: 6.64 us -> 0.02 us  [shards(): near = shifted(canvas[:, BAND:2 * BAND], 'win', 1)]
    ppermute x4 -> x2, starting transfers between devices: 10.7 us -> 5.17 us  [shifted(): return lax.ppermute(block, axis, route)]
    another operation x1 -> x0, loops' own time: 5.12 us -> none  [shards(): canvas, totals = lax.fori_loop(0, window_count, add_one, (canvas, totals))]
  transfers between devices with their start and end apart: 5 -> 2, of which waited for: 3 -> 2; matrix products, arithmetic and copies ran while one was open for 23% -> 0% of each run, Pallas kernels for 0% -> 0%
where the time goes in v1:
time: 80.6 us; the launch traced here: 80.3 us
  Pallas kernels  62 us (77%)
  waiting for transfers between devices  5.5 us (7%)
  starting transfers between devices  5.17 us (6%)
  local copies, waits for them, and re-layouts  4.88 us (6%)
  other arithmetic  1.76 us (2%)
  matrix products  0.88 us (1%)
    pallas_call x1, Pallas kernels, shards(): pl.pallas_call(functools.partial(block_kernel, n), out_shape=jax.ShapeDty...  62 us
    ppermute x2, waiting for transfers between devices, shifted(): return lax.ppermute(block, axis, route)  5.5 us
    ppermute x2, starting transfers between devices, shifted(): return lax.ppermute(block, axis, route)  5.17 us
    unnamed x3, local copies, waits for them, and re-layouts  2.16 us
  transfers between devices with their start and end apart: 2, of which 2 were waited for; matrix products, arithmetic and copies ran while one was open for 0% of the time, Pallas kernels for 0%

profile of v1, /device:TPU:8, one launch (start us, length us, event | category | flops | bytes accessed | tf_op | source)
XLA Modules:
  0.0 80.3 jit_solution(16135581804140836307)
XLA Ops:
  0.0 0.8 fusion.15
  0.8 2.2 %copy.14.wout_ref = bf16[3072,64]{1,0:T(8,128)(2,1)} copy(bf16[3072,64]{0,1:T(8,128)(2,1)} %param.12) | data formatting | bytes 786432 | tf_op args[4]
  2.9 62.0 %shard_map.82 = f32[512,64]{1,0:T(8,128)} custom-call(bf16[2,256,4608]{2,1,0:T(8,128)(2,1)} %qkv_hbm.1, bf16[2,128,3072]{2,1,0:T(8,128)(2,1)} %txt_hbm.1, bf16[512,3072]{1,0:T(8,128)(2,1)} %bitcast.23, bf16[96,3072]{1,0:T(8,128)(2,1)} %wp_hbm.1, bf16[3072,64]{1,0:T(8,128)(2,1)} %copy.14.wout_ref, f32[3,3072]{1,0:T(4,128)} %mod_ref.1), custom_call_target="tpu_custom_call" | custom-call | tf_op jit(solution)/shard_map/pallas_call | solution.py:369
  64.9 0.0 copy-start
  64.9 1.1 %copy.15 = f32[512,64]{0,1:T(8,128)S(1)} copy(f32[512,64]{1,0:T(8,128)} %shard_map.82) | data formatting | bytes 262144 | tf_op jit(solution)/shard_map/pallas_call | solution.py:369
  66.0 0.4 reshape.66
  66.4 0.8 copy.16
  67.2 0.5 copy.17
  67.7 0.0 copy-done
  67.7 0.2 subtract_reduce_fusion
  67.9 0.1 and_select_fusion
  68.0 0.4 fusion
  68.4 0.4 convolution_bitcast_fusion
  68.9 2.7 %collective-permute-start.1 = (f32[17,16,64]{2,1,0:T(8,128)S(1)}, f32[17,16,64]{2,1,0:T(8,128)S(1)}, u32[]{:S(2)}, u32[]{:S(2)}) collective-permute-start(f32[17,16,64]{2,1,0:T(8,128)S(1)} %get-tuple-element.8), channel_id=1, source_target_pairs={{0,2},{1,3},{2,4},{3,5},{4,6},{5,7},{6,8},{7,9},{8,10},{9,11},{10,... | collective-permute-start | bytes 208904 | tf_op jit(solution)/shard_map/ppermute | solution.py:24
  71.6 2.5 %collective-permute-start = (f32[17,16,64]{2,1,0:T(8,128)S(1)}, f32[17,16,64]{2,1,0:T(8,128)S(1)}, u32[]{:S(2)}, u32[]{:S(2)}) collective-permute-start(f32[17,16,64]{2,1,0:T(8,128)S(1)} %get-tuple-element.7), channel_id=1, source_target_pairs={{0,1},{1,2},{2,3},{3,4},{4,5},{5,6},{6,7},{7,8},{8,9},{9,10},{10,1... | collective-permute-start | bytes 208904 | tf_op jit(solution)/shard_map/ppermute | solution.py:24
  74.1 4.2 %collective-permute-done.1 = f32[17,16,64]{2,1,0:T(8,128)S(1)} collective-permute-done((f32[17,16,64]{2,1,0:T(8,128)S(1)}, f32[17,16,64]{2,1,0:T(8,128)S(1)}, u32[]{:S(2)}, u32[]{:S(2)}) %collective-permute-start.1) | collective-permute-done | bytes 69664 | tf_op jit(solution)/shard_map/ppermute | solution.py:24
  78.2 1.3 %collective-permute-done = f32[17,16,64]{2,1,0:T(8,128)S(1)} collective-permute-done((f32[17,16,64]{2,1,0:T(8,128)S(1)}, f32[17,16,64]{2,1,0:T(8,128)S(1)}, u32[]{:S(2)}, u32[]{:S(2)}) %collective-permute-start) | collective-permute-done | bytes 69664 | tf_op jit(solution)/shard_map/ppermute | solution.py:24
  79.6 0.7 slice_divide_fusion
  (4 shorter events, 0.1 us)
Async XLA Ops:
  64.9 2.8 %copy-start = (s32[2,2]{1,0:T(2,128)S(1)}, s32[2,2]{1,0:T(2,128)}, u32[]{:S(2)}) copy-start(s32[2,2]{1,0:T(2,128)} %param.14) | copy-start | bytes 52
  68.9 9.3 %collective-permute-start.1 = (f32[17,16,64]{2,1,0:T(8,128)S(1)}, f32[17,16,64]{2,1,0:T(8,128)S(1)}, u32[]{:S(2)}, u32[]{:S(2)}) collective-permute-start(f32[17,16,64]{2,1,0:T(8,128)S(1)} %get-tuple-element.8), channel_id=1, source_target_pairs={{0,2},{1,3},{2,4},{3,5},{4,6},{5,7},{6,8},{7,9},{8,10},{9,11},{10,... | collective-permute-start | bytes 208904 | tf_op jit(solution)/shard_map/ppermute | solution.py:24
  71.6 8.0 %collective-permute-start = (f32[17,16,64]{2,1,0:T(8,128)S(1)}, f32[17,16,64]{2,1,0:T(8,128)S(1)}, u32[]{:S(2)}, u32[]{:S(2)}) collective-permute-start(f32[17,16,64]{2,1,0:T(8,128)S(1)} %get-tuple-element.7), channel_id=1, source_target_pairs={{0,1},{1,2},{2,3},{3,4},{4,5},{5,6},{6,7},{7,8},{8,9},{9,10},{10,1... | collective-permute-start | bytes 208904 | tf_op jit(solution)/shard_map/ppermute | solution.py:24

commit v2 on v1

--- a/solution.py
+++ b/solution.py
@@ -208,10 +208,6 @@
             )
         )
     hid_load = pltpu.make_async_copy(hid_hbm, hid, load_sems.at[1 + 2 * windows])
-    for pair in loads:
-        for copy in pair:
-            copy.start()
-    hid_load.start()
 
     barrier = pltpu.get_barrier_semaphore()
     for device in (onward, backward, across, partner):
@@ -223,6 +219,10 @@
         cw(0, sub, 0).start()
         ccw(0, sub, 0).start()
     part_own(core).start()
+    for pair in loads:
+        for copy in pair:
+            copy.start()
+    hid_load.start()
 
     scale = LOG2E / math.sqrt(HD)
 
@@ -249,28 +249,30 @@
             out * (1.0 / total)
         ).astype(jnp.bfloat16)
 
-    tile = 256 if third % 256 == 0 else third
-
-    def project(left_chip, col, cols, first=False):
-        row = pl.multiple_of(left_chip * (2 * rows), 16)
-        lhs[...] = att[pl.ds(row, 2 * rows), :].T
+    tile = 512 if third % 512 == 0 else third
+
+    def project(held, col, first=False):
+        spots = [pl.ds(pl.multiple_of(q * (2 * rows), 16), 2 * rows) for q in held]
+        deep = 2 * rows * len(held)
+        lhs[:, :deep] = jnp.concatenate([att[spot, :] for spot in spots], axis=0).T
 
         def one(t, carry):
             at = pl.ds(pl.multiple_of(col + t * tile, 128), tile)
-            term = jnp.dot(
-                lhs[...], weights[pl.ds(row, 2 * rows), at], preferred_element_type=jnp.float32
-            )
+            rhs = jnp.concatenate([weights[spot, at] for spot in spots], axis=0)
+            term = jnp.dot(lhs[:, :deep], rhs, preferred_element_type=jnp.float32)
             acc[:, at] = term if first else acc[:, at] + term
             return carry
 
-        lax.fori_loop(0, cols // tile, one, 0)
-
-    def project_step(step):
-        for kind in range(3):
+        lax.fori_loop(0, third // tile, one, 0)
+
+    def project_kind(group_steps, kind, with_own=False):
+        for step in group_steps:
             part(step, kind, 1 - core).wait_recv()
-        project(chip_at(place - step - 1), own_third, third)
-        project(chip_at(place - step - 1), far_third, third)
-        project(chip_at(place + step + 1), third, third)
+        sign = 1 if kind == 1 else -1
+        held = [chip_at(place + sign * (step + 1)) for step in group_steps]
+        if with_own:
+            held = [chip] + held
+        project(held, (own_third, third, far_third)[kind], first=with_own)
 
     def serve(step, sub, more):
         cw(step, sub, 1).wait_recv()
@@ -315,20 +317,33 @@
         if step >= 1:
             hand_across(step - 1)
     part_own(1 - core).wait_recv()
-    project(chip, 0, width, first=True)
-    due = 0
+    opening = list(range(early - 1))
+    middle = list(range(early - 1, steps - 2))
+    closing = list(range(max(steps - 2, early - 1), steps))
+    work = [(opening, kind, True) for kind in (0, 2, 1)]
+    work += [None] * (2 * (steps - early) - 5)
+    if middle:
+        work += [(middle, kind, False) for kind in (0, 2, 1)]
     for step in range(early, steps):
         for sub in range(2):
-            if due <= step - 2:
-                project_step(due)
-                due += 1
+            quota = 1 if step < steps - 1 else 2
+            for _ in range(quota):
+                if work:
+                    piece = work.pop(0)
+                    if piece is not None:
+                        project_kind(*piece)
             serve(step, sub, step + 1 < steps)
         hand_over(step)
         hand_across(step - 1)
+    for piece in work:
+        if piece is not None:
+            project_kind(*piece)
+    for step in closing[:-1]:
+        for kind in range(3):
+            project_kind([step], kind)
     hand_across(steps - 1)
-    while due < steps:
-        project_step(due)
-        due += 1
+    for kind in (0, 1, 2):
+        project_kind(closing[-1:], kind)
 
     hid_load.wait()
     block = 64 if acc.shape[0] % 64 == 0 else acc.shape[0]
@@ -343,7 +358,9 @@
         centred = residual - mean
         var = jnp.sum(centred * centred, axis=-1, keepdims=True) * (1.0 / width)
         modulated = (centred * lax.rsqrt(var + 1e-06) * gain + shift).astype(jnp.bfloat16)
-        out_ref[at, :] = jnp.dot(modulated, wout_ref[...], preferred_element_type=jnp.float32)
+        out_ref[at, :] = lax.dot_general(
+            modulated, wout_ref[...], (((1,), (1,)), ((), ())), preferred_element_type=jnp.float32
+        )
         return carry
 
     lax.fori_loop(0, acc.shape[0] // block, norm, 0)
@@ -377,7 +394,7 @@
             pltpu.VMEM((total, width), jnp.bfloat16),
             pltpu.VMEM((n * rows, width), jnp.bfloat16),
             pltpu.VMEM((n * rows, total), jnp.bfloat16),
-            pltpu.VMEM((total, 2 * rows), jnp.bfloat16),
+            pltpu.VMEM((total, 2 * rows * (n // 4)), jnp.bfloat16),
             pltpu.VMEM((total, width), jnp.float32),
             dma((2 + 2 * windows,)),
             dma((steps, 2)),
@@ -393,7 +410,7 @@
         compiler_params=pltpu.CompilerParams(
             collective_id=0, has_side_effects=True, vmem_limit_bytes=60 * 1024 * 1024
         ),
-    )(img_qkv, txt_kv, hidden.reshape(total, width), w_proj, w_out, modulation)
+    )(img_qkv, txt_kv, hidden.reshape(total, width), w_proj, w_out.T, modulation)
 
     weights = blend_weight.astype(jnp.float32)
     grid = patch_vel.reshape(windows, GRID, GRID, C, PATCH, PATCH)

time: 80.6 us -> 65.9 us (0.82)
  Pallas kernels: 62 us -> 50.1 us
  local copies, waits for them, and re-layouts: 4.88 us -> 2.72 us
    pallas_call x1, Pallas kernels: 62 us -> 50.1 us  [shards(): pl.pallas_call(functools.partial(block_kernel, n), out_shape=jax.ShapeDty...]
    unnamed x3 -> x2, local copies, waits for them, and re-layouts: 2.16 us -> 0.01 us
where the time goes in v2:
time: 65.9 us; the launch traced here: 65.6 us
  Pallas kernels  50.1 us (76%)
  waiting for transfers between devices  5.48 us (8%)
  starting transfers between devices  4.5 us (7%)
  local copies, waits for them, and re-layouts  2.72 us (4%)
  other arithmetic  1.76 us (3%)
  matrix products  0.88 us (1%)
    pallas_call x1, Pallas kernels, shards(): pl.pallas_call(functools.partial(block_kernel, n), out_shape=jax.ShapeDty...  50.1 us
    ppermute x2, waiting for transfers between devices, shifted(): return lax.ppermute(block, axis, route)  5.48 us
    ppermute x2, starting transfers between devices, shifted(): return lax.ppermute(block, axis, route)  4.5 us
  transfers between devices with their start and end apart: 2, of which 2 were waited for; matrix products, arithmetic and copies ran while one was open for 0% of the time, Pallas kernels for 0%

profile of v2, /device:TPU:8, one launch (start us, length us, event | category | flops | bytes accessed | tf_op | source)
XLA Modules:
  0.0 65.6 jit_solution(6484816620638806310)
XLA Ops:
  0.0 0.8 %fusion.15 = (f32[2,32,32]{2,1,0:T(8,128)S(1)}, f32[2,1,32,32]{3,2,0,1:T(8,128)S(1)}) fusion(s32[2,32,32]{2,1,0:T(8,128)} %param.15), kind=kLoop, calls=%fused_computation.27 | loop fusion | flops 2048 | bytes 24576 | tf_op jit(solution)/shard_map/convert_element_type | solution.py:415
  0.8 50.1 %shard_map.82 = f32[512,64]{1,0:T(8,128)} custom-call(bf16[2,256,4608]{2,1,0:T(8,128)(2,1)} %qkv_hbm.1, bf16[2,128,3072]{2,1,0:T(8,128)(2,1)} %txt_hbm.1, bf16[512,3072]{1,0:T(8,128)(2,1)} %bitcast.24, bf16[96,3072]{1,0:T(8,128)(2,1)} %wp_hbm.1, bf16[64,3072]{1,0:T(8,128)(2,1)} %bitcast.25, f32[3,3072]{1,0:T(4,128)} %mod_ref.1), custom_call_target="tpu_custom_call" | custom-call | tf_op jit(solution)/shard_map/pallas_call | solution.py:386
  50.9 0.0 copy-start
  50.9 1.1 %copy.12 = f32[512,64]{0,1:T(8,128)S(1)} copy(f32[512,64]{1,0:T(8,128)} %shard_map.82) | data formatting | bytes 262144 | tf_op jit(solution)/shard_map/pallas_call | solution.py:386
  52.0 0.4 reshape.66
  52.4 0.8 %copy.13 = f32[2,16,16,2,16,2]{1,5,4,3,2,0:T(2,128)S(1)} copy(f32[2,16,16,2,16,2]{4,2,0,5,3,1:T(8,128)S(1)} %bitcast.22) | data formatting | bytes 262144 | tf_op jit(solution)/shard_map/transpose | solution.py:417
  53.2 0.5 copy.14
  53.7 0.0 copy-done
  53.7 0.2 subtract_reduce_fusion
  53.9 0.1 and_select_fusion
  54.0 0.4 fusion
  54.4 0.4 convolution_bitcast_fusion
  54.9 2.6 %collective-permute-start.1 = (f32[17,16,64]{2,1,0:T(8,128)S(1)}, f32[17,16,64]{2,1,0:T(8,128)S(1)}, u32[]{:S(2)}, u32[]{:S(2)}) collective-permute-start(f32[17,16,64]{2,1,0:T(8,128)S(1)} %get-tuple-element.8), channel_id=1, source_target_pairs={{0,2},{1,3},{2,4},{3,5},{4,6},{5,7},{6,8},{7,9},{8,10},{9,11},{10,... | collective-permute-start | bytes 208904 | tf_op jit(solution)/shard_map/ppermute | solution.py:24
  57.5 1.9 %collective-permute-start = (f32[17,16,64]{2,1,0:T(8,128)S(1)}, f32[17,16,64]{2,1,0:T(8,128)S(1)}, u32[]{:S(2)}, u32[]{:S(2)}) collective-permute-start(f32[17,16,64]{2,1,0:T(8,128)S(1)} %get-tuple-element.7), channel_id=1, source_target_pairs={{0,1},{1,2},{2,3},{3,4},{4,5},{5,6},{6,7},{7,8},{8,9},{9,10},{10,1... | collective-permute-start | bytes 208904 | tf_op jit(solution)/shard_map/ppermute | solution.py:24
  59.4 4.1 %collective-permute-done.1 = f32[17,16,64]{2,1,0:T(8,128)S(1)} collective-permute-done((f32[17,16,64]{2,1,0:T(8,128)S(1)}, f32[17,16,64]{2,1,0:T(8,128)S(1)}, u32[]{:S(2)}, u32[]{:S(2)}) %collective-permute-start.1) | collective-permute-done | bytes 69664 | tf_op jit(solution)/shard_map/ppermute | solution.py:24
  63.5 1.4 %collective-permute-done = f32[17,16,64]{2,1,0:T(8,128)S(1)} collective-permute-done((f32[17,16,64]{2,1,0:T(8,128)S(1)}, f32[17,16,64]{2,1,0:T(8,128)S(1)}, u32[]{:S(2)}, u32[]{:S(2)}) %collective-permute-start) | collective-permute-done | bytes 69664 | tf_op jit(solution)/shard_map/ppermute | solution.py:24
  64.9 0.7 %slice_divide_fusion = f32[16,16,64]{2,1,0:T(8,128)} fusion(f32[17,16,64]{2,1,0:T(8,128)S(1)} %fusion.4, f32[16,64]{1,0:T(8,128)S(1)} %fusion.11), kind=kLoop, calls=%fused_computation.8 | loop fusion | flops 16384 | bytes 135168 | tf_op jit(solution)/shard_map/div | solution.py:430
  (4 shorter events, 0.1 us)
Async XLA Ops:
  50.9 2.8 %copy-start = (s32[2,2]{1,0:T(2,128)S(1)}, s32[2,2]{1,0:T(2,128)}, u32[]{:S(2)}) copy-start(s32[2,2]{1,0:T(2,128)} %param.14) | copy-start | bytes 52
  54.9 8.6 %collective-permute-start.1 = (f32[17,16,64]{2,1,0:T(8,128)S(1)}, f32[17,16,64]{2,1,0:T(8,128)S(1)}, u32[]{:S(2)}, u32[]{:S(2)}) collective-permute-start(f32[17,16,64]{2,1,0:T(8,128)S(1)} %get-tuple-element.8), channel_id=1, source_target_pairs={{0,2},{1,3},{2,4},{3,5},{4,6},{5,7},{6,8},{7,9},{8,10},{9,11},{10,... | collective-permute-start | bytes 208904 | tf_op jit(solution)/shard_map/ppermute | solution.py:24
  57.5 7.4 %collective-permute-start = (f32[17,16,64]{2,1,0:T(8,128)S(1)}, f32[17,16,64]{2,1,0:T(8,128)S(1)}, u32[]{:S(2)}, u32[]{:S(2)}) collective-permute-start(f32[17,16,64]{2,1,0:T(8,128)S(1)} %get-tuple-element.7), channel_id=1, source_target_pairs={{0,1},{1,2},{2,3},{3,4},{4,5},{5,6},{6,7},{7,8},{8,9},{9,10},{10,1... | collective-permute-start | bytes 208904 | tf_op jit(solution)/shard_map/ppermute | solution.py:24

commit v3 on v2

--- a/solution.py
+++ b/solution.py
@@ -346,7 +346,7 @@
         project_kind(closing[-1:], kind)
 
     hid_load.wait()
-    block = 64 if acc.shape[0] % 64 == 0 else acc.shape[0]
+    block = 256 if acc.shape[0] % 256 == 0 else acc.shape[0]
     gate = mod_ref[0:1, :]
     gain = 1.0 + mod_ref[1:2, :]
     shift = mod_ref[2:3, :]
@@ -358,8 +358,8 @@
         centred = residual - mean
         var = jnp.sum(centred * centred, axis=-1, keepdims=True) * (1.0 / width)
         modulated = (centred * lax.rsqrt(var + 1e-06) * gain + shift).astype(jnp.bfloat16)
-        out_ref[at, :] = lax.dot_general(
-            modulated, wout_ref[...], (((1,), (1,)), ((), ())), preferred_element_type=jnp.float32
+        out_ref[:, pl.ds(pl.multiple_of(b * block, 128), block)] = lax.dot_general(
+            wout_ref[...], modulated, (((1,), (1,)), ((), ())), preferred_element_type=jnp.float32
         )
         return carry
 
@@ -385,7 +385,7 @@
     dma = pltpu.SemaphoreType.DMA
     patch_vel = pl.pallas_call(
         functools.partial(block_kernel, n),
-        out_shape=jax.ShapeDtypeStruct((total, w_out.shape[1]), jnp.float32),
+        out_shape=jax.ShapeDtypeStruct((w_out.shape[1], total), jnp.float32),
         in_specs=[any_space] * 4 + [vmem] * 2,
         out_specs=vmem,
         scratch_shapes=[
@@ -413,8 +413,8 @@
     )(img_qkv, txt_kv, hidden.reshape(total, width), w_proj, w_out.T, modulation)
 
     weights = blend_weight.astype(jnp.float32)
-    grid = patch_vel.reshape(windows, GRID, GRID, C, PATCH, PATCH)
-    window_vel = grid.transpose(0, 3, 1, 4, 2, 5).reshape(windows, C, WIN, WIN)
+    grid = patch_vel.reshape(C, PATCH, PATCH, windows, GRID, GRID)
+    window_vel = grid.transpose(3, 0, 4, 1, 5, 2).reshape(windows, C, WIN, WIN)
     contrib = jnp.concatenate([window_vel * weights[:, None], weights[:, None]], axis=1)
     band_start = lax.axis_index("win") * BAND
     cells = jnp.arange(WIN, dtype=jnp.int32)

time: 65.9 us -> 64.3 us (0.976)
  Pallas kernels: 50.1 us -> 48.8 us
    reshape x2 -> x3, local copies, waits for them, and re-layouts: 0.83 us -> 2.54 us  [the longest x2 2.07 us: shards(): grid = patch_vel.reshape(C, PATCH, PATCH, windows, GRID, GRID)]
    pallas_call x1, Pallas kernels: 50.1 us -> 48.8 us  [shards(): pl.pallas_call(functools.partial(block_kernel, n), out_shape=jax.ShapeDty...]
    pallas_call x1 -> x0, local copies, waits for them, and re-layouts: 1.07 us -> none  [shards(): pl.pallas_call(functools.partial(block_kernel, n), out_shape=jax.ShapeDty...]
    transpose x1 -> x0, local copies, waits for them, and re-layouts: 0.8 us -> none  [shards(): window_vel = grid.transpose(0, 3, 1, 4, 2, 5).reshape(windows, C, WIN, WIN)]
where the time goes in v3:
time: 64.3 us; the launch traced here: 64.1 us
  Pallas kernels  48.8 us (76%)
  waiting for transfers between devices  5.48 us (9%)
  starting transfers between devices  4.5 us (7%)
  local copies, waits for them, and re-layouts  2.57 us (4%)
  other arithmetic  1.76 us (3%)
  matrix products  0.88 us (1%)
    pallas_call x1, Pallas kernels, shards(): pl.pallas_call(functools.partial(block_kernel, n), out_shape=jax.ShapeDty...  48.8 us
    ppermute x2, waiting for transfers between devices, shifted(): return lax.ppermute(block, axis, route)  5.48 us
    ppermute x2, starting transfers between devices, shifted(): return lax.ppermute(block, axis, route)  4.5 us
    reshape x2, local copies, waits for them, and re-layouts, shards(): grid = patch_vel.reshape(C, PATCH, PATCH, windows, GRID, GRID)  2.07 us
  transfers between devices with their start and end apart: 2, of which 2 were waited for; matrix products, arithmetic and copies ran while one was open for 0% of the time, Pallas kernels for 0%

profile of v3, /device:TPU:8, one launch (start us, length us, event | category | flops | bytes accessed | tf_op | source)
XLA Modules:
  0.0 64.1 jit_solution(7487268100928794369)
XLA Ops:
  0.0 0.8 %fusion.15 = (f32[2,32,32]{2,1,0:T(8,128)S(1)}, f32[2,1,32,32]{3,2,0,1:T(8,128)S(1)}) fusion(s32[2,32,32]{2,1,0:T(8,128)} %param.15), kind=kLoop, calls=%fused_computation.27 | loop fusion | flops 2048 | bytes 24576 | tf_op jit(solution)/shard_map/convert_element_type | solution.py:415
  0.8 48.8 %shard_map.82 = f32[64,512]{1,0:T(8,128)} custom-call(bf16[2,256,4608]{2,1,0:T(8,128)(2,1)} %qkv_hbm.1, bf16[2,128,3072]{2,1,0:T(8,128)(2,1)} %txt_hbm.1, bf16[512,3072]{1,0:T(8,128)(2,1)} %bitcast.22, bf16[96,3072]{1,0:T(8,128)(2,1)} %wp_hbm.1, bf16[64,3072]{1,0:T(8,128)(2,1)} %bitcast.23, f32[3,3072]{1,0:T(4,128)} %mod_ref.1), custom_call_target="tpu_custom_call" | custom-call | tf_op jit(solution)/shard_map/pallas_call | solution.py:386
  49.5 0.0 copy-start
  49.6 1.3 %reshape.66 = f32[16,2,2,2,16,16]{5,4,3,2,1,0:T(8,128)S(1)} reshape(f32[64,512]{1,0:T(8,128)} %shard_map.82) | data formatting | bytes 262144 | tf_op jit(solution)/shard_map/reshape | solution.py:416
  50.8 0.8 %copy.11 = f32[16,2,2,2,16,16]{0,2,5,1,4,3:T(2,128)S(1)} copy(f32[16,2,2,2,16,16]{5,4,3,2,1,0:T(8,128)S(1)} %reshape.66) | data formatting | bytes 262144 | tf_op jit(solution)/shard_map/reshape | solution.py:416
  51.6 0.5 copy.12
  52.2 0.0 copy-done
  52.2 0.2 subtract_reduce_fusion
  52.4 0.1 and_select_fusion
  52.4 0.4 fusion
  52.9 0.4 convolution_bitcast_fusion
  53.4 2.6 %collective-permute-start.1 = (f32[17,16,64]{2,1,0:T(8,128)S(1)}, f32[17,16,64]{2,1,0:T(8,128)S(1)}, u32[]{:S(2)}, u32[]{:S(2)}) collective-permute-start(f32[17,16,64]{2,1,0:T(8,128)S(1)} %get-tuple-element.8), channel_id=1, source_target_pairs={{0,2},{1,3},{2,4},{3,5},{4,6},{5,7},{6,8},{7,9},{8,10},{9,11},{10,... | collective-permute-start | bytes 208904 | tf_op jit(solution)/shard_map/ppermute | solution.py:24
  56.0 1.9 %collective-permute-start = (f32[17,16,64]{2,1,0:T(8,128)S(1)}, f32[17,16,64]{2,1,0:T(8,128)S(1)}, u32[]{:S(2)}, u32[]{:S(2)}) collective-permute-start(f32[17,16,64]{2,1,0:T(8,128)S(1)} %get-tuple-element.7), channel_id=1, source_target_pairs={{0,1},{1,2},{2,3},{3,4},{4,5},{5,6},{6,7},{7,8},{8,9},{9,10},{10,1... | collective-permute-start | bytes 208904 | tf_op jit(solution)/shard_map/ppermute | solution.py:24
  57.9 4.1 %collective-permute-done.1 = f32[17,16,64]{2,1,0:T(8,128)S(1)} collective-permute-done((f32[17,16,64]{2,1,0:T(8,128)S(1)}, f32[17,16,64]{2,1,0:T(8,128)S(1)}, u32[]{:S(2)}, u32[]{:S(2)}) %collective-permute-start.1) | collective-permute-done | bytes 69664 | tf_op jit(solution)/shard_map/ppermute | solution.py:24
  62.0 1.4 %collective-permute-done = f32[17,16,64]{2,1,0:T(8,128)S(1)} collective-permute-done((f32[17,16,64]{2,1,0:T(8,128)S(1)}, f32[17,16,64]{2,1,0:T(8,128)S(1)}, u32[]{:S(2)}, u32[]{:S(2)}) %collective-permute-start) | collective-permute-done | bytes 69664 | tf_op jit(solution)/shard_map/ppermute | solution.py:24
  63.4 0.7 %slice_divide_fusion = f32[16,16,64]{2,1,0:T(8,128)} fusion(f32[17,16,64]{2,1,0:T(8,128)S(1)} %fusion.4, f32[16,64]{1,0:T(8,128)S(1)} %fusion.11), kind=kLoop, calls=%fused_computation.8 | loop fusion | flops 16384 | bytes 135168 | tf_op jit(solution)/shard_map/div | solution.py:430
  (4 shorter events, 0.1 us)
Async XLA Ops:
  49.5 2.6 %copy-start = (s32[2,2]{1,0:T(2,128)S(1)}, s32[2,2]{1,0:T(2,128)}, u32[]{:S(2)}) copy-start(s32[2,2]{1,0:T(2,128)} %param.14) | copy-start | bytes 52
  53.4 8.6 %collective-permute-start.1 = (f32[17,16,64]{2,1,0:T(8,128)S(1)}, f32[17,16,64]{2,1,0:T(8,128)S(1)}, u32[]{:S(2)}, u32[]{:S(2)}) collective-permute-start(f32[17,16,64]{2,1,0:T(8,128)S(1)} %get-tuple-element.8), channel_id=1, source_target_pairs={{0,2},{1,3},{2,4},{3,5},{4,6},{5,7},{6,8},{7,9},{8,10},{9,11},{10,... | collective-permute-start | bytes 208904 | tf_op jit(solution)/shard_map/ppermute | solution.py:24
  56.0 7.4 %collective-permute-start = (f32[17,16,64]{2,1,0:T(8,128)S(1)}, f32[17,16,64]{2,1,0:T(8,128)S(1)}, u32[]{:S(2)}, u32[]{:S(2)}) collective-permute-start(f32[17,16,64]{2,1,0:T(8,128)S(1)} %get-tuple-element.7), channel_id=1, source_target_pairs={{0,1},{1,2},{2,3},{3,4},{4,5},{5,6},{6,7},{7,8},{8,9},{9,10},{10,1... | collective-permute-start | bytes 208904 | tf_op jit(solution)/shard_map/ppermute | solution.py:24
